TPU v7x, 32 devices: a whole 2x2x4 slice. The times are simulated.
32 devices in a mesh: band: 4 (over z), sector: 8 (over y, x, core).
Axes of the slice: x: 2, y: 2, z: 4, core: 2. Of those that a mesh axis runs over, the one named last changes fastest.
Arguments:
- field: float32 [2, 640, 2, 2560], P(None, 'band', None, 'sector'), may hold values from -6 to 6
- depart: int32 [2, 640, 80], P(None, 'band', 'sector'), may hold values from -2 to 2
- interp_weight: bfloat16 [2, 640, 80, 64, 32], P(None, 'band', 'sector'), may hold values from -0.75 to 0.75
- legendre: float32 [640, 640, 1281], P('sector', 'band'), may hold values from -0.25 to 0.25
- damping: float32 [2], replicated, may hold values from 0.3 to 30
Outputs:
- new_field: float32 [2, 640, 2, 2560], P(None, 'band', None, 'sector')
All inputs are finite; a program needn't handle non-finite values.
Results may differ from a plain program's by a relative error of at most 0.0003.
Values sent between devices are 32-bit elements; how exact they have to be, the bound alone decides.
No kernel may reach another device: no remote copies, remote signals or barrier semaphores. Data moves between devices by JAX's collectives and lax.ppermute only.
A program may use at most 192 MiB of HBM per device.

v0:
```python
import math
import jax
import jax.numpy as jnp
from jax import lax
from jax.sharding import PartitionSpec as P

HIGHEST = lax.Precision.HIGHEST


def padded(x, sides, width):
    for axis, dim in sides:
        peers, length = (lax.axis_size(axis), x.shape[dim])
        up = [(i, (i + 1) % peers) for i in range(peers)]
        down = [(j, i) for i, j in up]
        last = lax.slice_in_dim(x, length - width, length, axis=dim)
        leading = lax.slice_in_dim(x, 0, width, axis=dim)
        before = lax.ppermute(last, axis, up)
        after = lax.ppermute(leading, axis, down)
        x = jnp.concatenate([before, x, after], axis=dim)
    return x


def phase(product, lon_count):
    return 2.0 * math.pi / lon_count * (product % lon_count).astype(jnp.float32)


def forward_table(lon_count, m_count, pair_total):
    longitude = jnp.arange(lon_count, dtype=jnp.int32)[:, None]
    pair_range = jnp.arange(pair_total, dtype=jnp.int32)[None, :]
    lower_angle = phase(longitude * pair_range, lon_count)
    upper_angle = phase(longitude * (m_count - 1 - pair_range), lon_count)
    table = jnp.stack(
        [jnp.cos(lower_angle), -jnp.sin(lower_angle), jnp.cos(upper_angle), -jnp.sin(upper_angle)],
        axis=1,
    )
    return table / lon_count


def inverse_table(lon_count, m_count, pair_total):
    pair_range = jnp.arange(pair_total, dtype=jnp.int32)[:, None]
    longitude = jnp.arange(lon_count, dtype=jnp.int32)[None, :]
    lower_angle = phase(pair_range * longitude, lon_count)
    upper_angle = phase((m_count - 1 - pair_range) * longitude, lon_count)
    lower_scale = jnp.where(pair_range == 0, 1.0, 2.0)
    return jnp.stack(
        [
            lower_scale * jnp.cos(lower_angle),
            -lower_scale * jnp.sin(lower_angle),
            2.0 * jnp.cos(upper_angle),
            -2.0 * jnp.sin(upper_angle),
        ],
        axis=0,
    )


def pair_masks(pair_index, m_count, row_count):
    column = jnp.arange(row_count, dtype=jnp.int32)[None, :]
    limit = (m_count - pair_index)[:, None]
    leading = column < limit
    lag_value = jnp.where(leading, column, column - limit)
    odd_rows = lag_value % 2 == 1
    degree = jnp.where(leading, pair_index[:, None] + column, column - 1)
    return (leading, odd_rows, degree)


def analyse(wave, legendre, leading, odd_rows):
    stacked = jnp.stack([wave[0] + wave[1], wave[0] - wave[1]])
    product = jnp.einsum("svcpl,plk->svcpk", stacked, legendre, precision=HIGHEST)
    chosen = jnp.where(odd_rows, product[1], product[0])
    return jnp.where(leading, chosen[:, 0:2], chosen[:, 2:4])


def solve_modes(spectrum, damping_levels, degree, m_count):
    ratio = (degree * (degree + 1)).astype(jnp.float32) / float(m_count * m_count)
    return spectrum / (1.0 + damping_levels[:, None, None, None] * ratio[None, None])


def synthesise(spectrum, legendre, leading, odd_rows):
    lower = jnp.where(leading, spectrum, 0.0)
    upper = jnp.where(leading, 0.0, spectrum)
    northern = jnp.concatenate([lower, upper], axis=1)
    southern = jnp.where(odd_rows, -northern, northern)
    stacked = jnp.stack([northern, southern])
    return jnp.einsum("hvcpk,plk->hvcpl", stacked, legendre, precision=HIGHEST)


def advect(field, depart, interp_weight):
    tile_width = interp_weight.shape[-1]
    tile_count = depart.shape[2]
    extended = padded(field, (("sector", 3),), 3 * tile_width)
    pieces = extended.reshape(
        field.shape[0], field.shape[1], field.shape[2], tile_count + 6, tile_width
    )
    window = jnp.zeros(field.shape[:3] + (tile_count, 2 * tile_width), jnp.float32)
    for offset in range(-2, 3):
        lead_part = pieces[:, :, :, 3 + offset : 3 + offset + tile_count]
        next_part = pieces[:, :, :, 4 + offset : 4 + offset + tile_count]
        candidate = jnp.concatenate([lead_part, next_part], axis=4)
        window = jnp.where((depart == offset)[:, :, None, :, None], candidate, window)
    result = jnp.einsum(
        "hlvtj,hltji->hlvti", window, interp_weight.astype(jnp.float32), precision=HIGHEST
    )
    return result.reshape(field.shape)


def local(field, depart, interp_weight, legendre, damping):
    advected = advect(field, depart, interp_weight)
    columns = lax.all_to_all(advected, "sector", split_axis=1, concat_axis=3, tiled=True)
    lon_count = columns.shape[3]
    row_count = legendre.shape[2]
    m_count = row_count - 1
    pair_total = m_count // 2
    fourier = jnp.einsum(
        "hlvn,ncp->hvcpl", columns, forward_table(lon_count, m_count, pair_total), precision=HIGHEST
    )
    wave = lax.all_to_all(fourier, "sector", split_axis=3, concat_axis=4, tiled=True)
    pair_local = legendre.shape[0]
    pair_index = lax.axis_index("sector") * pair_local + jnp.arange(pair_local, dtype=jnp.int32)
    leading, odd_rows, degree = pair_masks(pair_index, m_count, row_count)
    partial_value = analyse(wave, legendre, leading, odd_rows)
    summed = lax.psum(partial_value, "band")
    spectrum = solve_modes(summed, damping, degree, m_count)
    synthesis = synthesise(spectrum, legendre, leading, odd_rows)
    returned = lax.all_to_all(synthesis, "sector", split_axis=4, concat_axis=3, tiled=True)
    gridded = jnp.einsum(
        "hvcpl,cpn->hlvn",
        returned,
        inverse_table(lon_count, m_count, pair_total),
        precision=HIGHEST,
    )
    return lax.all_to_all(gridded, "sector", split_axis=3, concat_axis=1, tiled=True)


def solution(mesh):
    return jax.shard_map(
        local,
        mesh=mesh,
        in_specs=(
            P(None, "band", None, "sector"),
            P(None, "band", "sector"),
            P(None, "band", "sector", None, None),
            P("sector", "band", None),
            P(),
        ),
        out_specs=P(None, "band", None, "sector"),
        check_vma=False,
    )
```

profile of v0, /device:TPU:0, one launch (start us, length us, event | category | flops | bytes accessed | tf_op | source)
XLA Modules:
  0.0 574.6 jit_solution(14221418994076441532)
XLA Ops:
  8.7 2.9 collective-permute-start.1
  11.6 28.4 %fusion.32 = (f32[2560,1,640]{2,0,1:T(8,128)}, f32[2560,1,640]{2,0,1:T(8,128)}) fusion(s32[640]{0:T(1024)S(1)} %iota_subtract_fusion), kind=kLoop, calls=%fused_computation.40 | loop fusion | flops 16384000 | bytes 13109760 | tf_op jit(solution)/shard_map/cos | solution.py:33
  40.2 47.9 %copy.114 = bf16[2,160,10,64,32]{3,4,2,1,0:T(8,128)(2,1)} copy(bf16[2,160,10,64,32]{1,4,3,2,0:T(8,128)(2,1)} %param.7) | data formatting | bytes 26214400 | tf_op args[2]
  91.1 3.6 copy.113
  94.7 43.8 %convolution_bitcast_fusion = f32[2,160,2,10,32]{4,2,3,1,0:T(2,128)S(1)} fusion(f32[2,160,2,10,64]{4,2,3,1,0:T(2,128)} %copy.113, bf16[2,160,10,64,32]{3,4,2,1,0:T(8,128)(2,1)} %copy.114), kind=kOutput, calls=%fused_computation.67 | convolution fusion | flops 157286400 | bytes 15564800 | tf_op jit(solution)/shard_map/hlvtj,hltji->hlvti/dot_general | solution.py:100
  138.4 3.4 copy.115
  144.2 4.0 all-to-all-start
  148.2 27.9 %sine_negate_fusion.1 = (f32[2560,1,640]{2,0,1:T(8,128)}, f32[2560,1,640]{2,0,1:T(8,128)}) fusion(), kind=kLoop, calls=%fused_computation.41 | loop fusion | flops 16384000 | bytes 13107200 | tf_op jit(solution)/shard_map/neg | solution.py:33
  176.7 19.3 %fusion.54 = f32[2,2,4,640,20]{3,4,1,0,2:T(8,128)S(1)} fusion(f32[2,20,2,2560,1]{3,1,2,0,4:T(8,128)S(1)} %reshape.528, f32[2560,1,640]{2,0,1:T(8,128)} %get-tuple-element.25, f32[2560,1,640]{2,0,1:T(8,128)} %get-tuple-element.24, f32[2560,1,640]{2,0,1:T(8,128)} %get-tuple-element.30, f32[2560,1,640]{2,0,1:T(8,128)} %get-tuple-element.31), kind=kOutput, calls=%fused_computation.78 | convolution fusion | flops 6317670400 | bytes 27852800 | tf_op jit(solution)/shard_map/hlvn,ncp->hvcpl/dot_general | solution.py:113
  196.0 5.0 copy.120
  201.0 10.6 %reshape.535 = f32[8,1,25600]{2,1,0:T(1,128)} reshape(f32[640,4,2,2,20]{4,3,2,1,0:T(2,128)} %bitcast.90) | data formatting | bytes 1638400
  211.6 4.2 all-to-all-start.1
  217.1 11.6 %all-to-all-done.1 = f32[8,1,25600]{2,1,0:T(1,128)S(1)} async-done(((f32[8,1,25600]{2,1,0:T(1,128)}), f32[8,1,25600]{2,1,0:T(1,128)S(1)}, u32[]{:S(2)}, u32[]{:S(2)}) %all-to-all-start.1) | async-done | bytes 819232 | tf_op jit(solution)/shard_map/all_to_all | solution.py:116
  229.2 2.6 reduce
  231.8 10.9 %reshape.536 = f32[640,4,2,2,20]{4,3,2,1,0:T(2,128)} reshape(f32[8,25600]{1,0:T(8,128)S(1)} %reduce) | data formatting | bytes 1638400
  242.7 6.0 %copy.141 = f32[2,2,4,8,80,20]{4,3,2,5,1,0:T(8,128)S(1)} copy(f32[2,2,4,8,80,20]{5,1,0,2,4,3:T(2,128)} %bitcast.91) | data formatting | bytes 1638400 | tf_op jit(solution)/shard_map/all_to_all | solution.py:116
  250.4 42.7 %fusion.44 = f32[2,2,4,80,1281]{4,2,1,0,3:T(4,128)} fusion(f32[80,160,1281]{2,1,0:T(8,128)} %param.8, f32[2,2,4,80,160]{4,2,1,0,3:T(4,128)S(1)} %fusion.83), kind=kOutput, calls=%fused_computation.61 | convolution fusion | flops 3148185600 | bytes 72965120 | tf_op jit(solution)/shard_map/svcpl,plk->svcpk/dot_general | solution.py:68
  293.2 4.5 fusion.48
  297.6 2.6 slice_select_fusion
  300.8 28.3 %sine_multiply_fusion.1 = (f32[1,640,2560]{2,1,0:T(8,128)}, f32[1,640,2560]{2,1,0:T(8,128)}) fusion(f32[640]{0:T(1024)S(1)} %fusion.65, f32[640]{0:T(1024)S(1)} %fusion.64), kind=kLoop, calls=%fused_computation.51 | loop fusion | flops 18022400 | bytes 13112320 | tf_op jit(solution)/shard_map/mul | solution.py:48
  329.0 48.0 %all-reduce.2.cloned.1.call-done = f32[2,2,80,1281]{3,1,0,2:T(2,128)} async-done(((f32[2,2,80,1281]{3,1,0,2:T(2,128)}), f32[2,2,80,1281]{3,1,0,2:T(2,128)}) %all-reduce.2.cloned.1.call-update) | async-done | bytes 1639696 | tf_op jit(solution)/shard_map/psum | solution.py:121
  377.0 3.1 broadcast_select_fusion.1
  386.5 73.3 %fusion.49 = f32[2,2,4,80,160]{4,2,1,0,3:T(4,128)S(1)} fusion(f32[80,160,1281]{2,1,0:T(8,128)} %param.8, f32[1,2,4,80,1281]{4,2,1,3,0:T(4,128)S(1)} %negate_select_fusion, f32[1,2,4,80,1281]{4,2,1,3,0:T(4,128)S(1)} %maximum_bitcast_fusion.4), kind=kOutput, calls=%fused_computation.77 | convolution fusion | flops 3149825280 | bytes 72965120 | tf_op jit(solution)/shard_map/hvcpk,plk->hvcpl/dot_general | solution.py:84
  461.4 4.1 all-to-all-start.2
  465.6 29.7 %cosine_multiply_fusion = (f32[1,640,2560]{2,1,0:T(8,128)}, f32[1,640,2560]{2,1,0:T(8,128)}) fusion(s32[640]{0:T(1024)S(1)} %iota_subtract_fusion), kind=kLoop, calls=%fused_computation.47 | loop fusion | flops 18022400 | bytes 13109760 | tf_op jit(solution)/shard_map/mul | solution.py:49
  496.5 19.2 %fusion.47 = f32[2,20,2,2560]{3,1,2,0:T(8,128)S(1)} fusion(f32[2,2,4,640,20]{3,4,2,1,0:T(8,128)S(1)} %reshape.534, f32[1,640,2560]{2,1,0:T(8,128)} %get-tuple-element.23, f32[1,640,2560]{2,1,0:T(8,128)} %get-tuple-element.22, f32[1,640,2560]{2,1,0:T(8,128)} %get-tuple-element.32, f32[1,640,2560]{2,1,0:T(8,128)} %get-tuple-element.33), kind=kOutput, calls=%fused_computation.62 | convolution fusion | flops 6311116800 | bytes 27852800 | tf_op jit(solution)/shard_map/hvcpl,cpn->hlvn/dot_general | solution.py:125
  515.7 5.0 copy.132
  520.7 9.9 %reshape.537 = f32[8,1,25600]{2,1,0:T(1,128)S(1)} reshape(f32[2560,2,2,20]{3,2,1,0:T(2,128)} %bitcast.92) | data formatting | bytes 1638400
  530.6 17.1 %all_to_all.69 = f32[8,1,25600]{2,1,0:T(1,128)S(1)} all-to-all(f32[8,1,25600]{2,1,0:T(1,128)S(1)} %reshape.537), channel_id=1, replica_groups=mesh['band'=4,'sector'=8] {'sector'}, dimensions={0} | all-to-all | bytes 1638400 | tf_op jit(solution)/shard_map/all_to_all | solution.py:131
  547.7 2.6 reduce.1
  550.3 10.9 %reshape.538 = f32[2560,2,2,20]{3,2,1,0:T(2,128)} reshape(f32[8,25600]{1,0:T(8,128)S(1)} %reduce.1) | data formatting | bytes 1638400
  561.1 5.0 copy.144
  (50 shorter events, 22.8 us)
Async XLA Ops:
  8.2 79.9 %collective-permute-start = (f32[2,160,2,96]{1,3,2,0:T(8,128)S(1)}, f32[2,160,2,96]{1,3,2,0:T(8,128)S(1)}, u32[]{:S(2)}, u32[]{:S(2)}) collective-permute-start(f32[2,160,2,96]{1,3,2,0:T(8,128)S(1)} %get-tuple-element.15), channel_id=1, source_target_pairs={{0,1},{1,2},{2,3},{3,4},{4,5},{5,6},{6,7},{7,0},{8,9},{9,10},{10,1... | collective-permute-start | bytes 737288 | tf_op jit(solution)/shard_map/ppermute | solution.py:17
  8.7 79.4 %collective-permute-start.1 = (f32[2,160,2,96]{1,3,2,0:T(8,128)S(1)}, f32[2,160,2,96]{1,3,2,0:T(8,128)S(1)}, u32[]{:S(2)}, u32[]{:S(2)}) collective-permute-start(f32[2,160,2,96]{1,3,2,0:T(8,128)S(1)} %get-tuple-element.16), channel_id=1, source_target_pairs={{1,0},{2,1},{3,2},{4,3},{5,4},{6,5},{7,6},{0,7},{9,8},{10,9},{11,1... | collective-permute-start | bytes 737288 | tf_op jit(solution)/shard_map/ppermute | solution.py:18
  11.6 28.4 %copy-start.1 = (s32[2,160,10]{1,0,2:T(2,128)S(1)}, s32[2,160,10]{1,0,2:T(2,128)}, u32[]{:S(2)}) copy-start(s32[2,160,10]{1,0,2:T(2,128)} %param.6) | copy-start | bytes 38404
  144.2 31.9 %all-to-all-start = ((f32[2,160,2,320]{3,2,0,1:T(2,128)}), f32[2,160,2,320]{3,2,0,1:T(2,128)S(1)}, u32[]{:S(2)}, u32[]{:S(2)}) async-start(f32[2,160,2,320]{3,2,0,1:T(2,128)} %copy.116), calls=%async_computation | async-start | bytes 1966080 | tf_op jit(solution)/shard_map/all_to_all | solution.py:108
  211.6 17.1 %all-to-all-start.1 = ((f32[8,1,25600]{2,1,0:T(1,128)}), f32[8,1,25600]{2,1,0:T(1,128)S(1)}, u32[]{:S(2)}, u32[]{:S(2)}) async-start(f32[8,1,25600]{2,1,0:T(1,128)} %reshape.535), calls=%async_computation.1 | async-start | bytes 1638400 | tf_op jit(solution)/shard_map/all_to_all | solution.py:116
  215.8 161.2 %all-reduce.2.cloned.1.call-start = ((), (), s32[]{:S(2)}) async-start(), calls=%async_computation.4 | async-start | bytes 3604480 | tf_op jit(solution)/shard_map/psum | solution.py:121
  250.4 42.8 %copy-start = (pred[80,1281]{1,0:T(8,128)(4,1)S(1)}, pred[80,1281]{1,0:T(8,128)(4,1)}, u32[]{:S(2)}) copy-start(pred[80,1281]{1,0:T(8,128)(4,1)} %get-tuple-element.26) | copy-start | bytes 307444
  297.6 2.7 copy-start.2
  461.4 33.8 %all-to-all-start.2 = ((f32[2,2,4,80,160]{3,2,1,0,4:T(4,128)}), f32[2,2,4,80,160]{3,2,1,0,4:T(4,128)S(1)}, u32[]{:S(2)}, u32[]{:S(2)}) async-start(f32[2,2,4,80,160]{3,2,1,0,4:T(4,128)} %copy.128), calls=%async_computation.2 | async-start | bytes 2621440 | tf_op jit(solution)/shard_map/all_to_all | solution.py:124
Sparse Core Ops, SparseCore 0:
  300.4 76.5 all-reduce.1
where the time goes:
time: 584 us; the launch traced here: 575 us
  matrix products  198 us (34%)
  other arithmetic  140 us (24%)
  local copies, waits for them, and re-layouts  130 us (22%)
  waiting for transfers between devices  59.6 us (10%)
  blocking collectives  17.1 us (3%)
  starting transfers between devices  15.9 us (3%)
  between operations  13.9 us (2%)
    unnamed x12, local copies, waits for them, and re-layouts  91.7 us
    dot_general x1, matrix products, synthesise(): return jnp.einsum('hvcpk,plk->hvcpl', stacked, legendre, precision=HIGHEST)  73.3 us
    psum x1, waiting for transfers between devices, local(): summed = lax.psum(partial_value, 'band')  48 us
    dot_general x1, matrix products, advect(): jnp.einsum('hlvtj,hltji->hlvti', window, interp_weight.astype(jnp.float32...  43.8 us
    dot_general x1, matrix products, analyse(): jnp.einsum('svcpl,plk->svcpk', stacked, legendre, precision=HIGHEST)  42.7 us
    mul x1, other arithmetic, inverse_table(): 2.0 * jnp.cos(upper_angle)  29.7 us
    cos x1, other arithmetic, forward_table(): jnp.cos(upper_angle)  28.4 us
    mul x1, other arithmetic, inverse_table(): -lower_scale * jnp.sin(lower_angle)  28.3 us
  transfers between devices with their start and end apart: 6, of which 2 were waited for; matrix products, arithmetic and copies ran while one was open for 29% of the time, Pallas kernels for 0%

commit v1 on v0

--- a/solution.py
+++ b/solution.py
@@ -118,7 +118,7 @@
     pair_index = lax.axis_index("sector") * pair_local + jnp.arange(pair_local, dtype=jnp.int32)
     leading, odd_rows, degree = pair_masks(pair_index, m_count, row_count)
     partial_value = analyse(wave, legendre, leading, odd_rows)
-    summed = lax.psum(partial_value, "band")
+    summed = jnp.sum(lax.all_gather(partial_value, "band"), axis=0)
     spectrum = solve_modes(summed, damping, degree, m_count)
     synthesis = synthesise(spectrum, legendre, leading, odd_rows)
     returned = lax.all_to_all(synthesis, "sector", split_axis=4, concat_axis=3, tiled=True)

time: 584 us -> 644 us (1.10)
  waiting for transfers between devices: 59.6 us -> 114 us
    all_gather x0 -> x1, waiting for transfers between devices: none -> 101 us  [local(): summed = jnp.sum(lax.all_gather(partial_value, 'band'), axis=0)]
    psum x1 -> x0, waiting for transfers between devices: 48 us -> none  [local(): summed = lax.psum(partial_value, 'band')]
    reduce_sum x0 -> x1, other arithmetic: none -> 7.08 us  [local(): summed = jnp.sum(lax.all_gather(partial_value, 'band'), axis=0)]
    unnamed x12 -> x10, local copies, waits for them, and re-layouts: 91.7 us -> 91.8 us
  transfers between devices with their start and end apart: 6 -> 6, of which waited for: 2 -> 2; matrix products, arithmetic and copies ran while one was open for 29% -> 26% of each run, Pallas kernels for 0% -> 0%
where the time goes in v1:
time: 644 us; the launch traced here: 634 us
  matrix products  198 us (31%)
  other arithmetic  145 us (23%)
  local copies, waits for them, and re-layouts  130 us (20%)
  waiting for transfers between devices  114 us (18%)
  blocking collectives  17.2 us (3%)
  starting transfers between devices  15.4 us (2%)
  between operations  14.3 us (2%)
    all_gather x1, waiting for transfers between devices, local(): summed = jnp.sum(lax.all_gather(partial_value, 'band'), axis=0)  101 us
    unnamed x10, local copies, waits for them, and re-layouts  91.8 us
    dot_general x1, matrix products, synthesise(): return jnp.einsum('hvcpk,plk->hvcpl', stacked, legendre, precision=HIGHEST)  73.2 us
    dot_general x1, matrix products, advect(): jnp.einsum('hlvtj,hltji->hlvti', window, interp_weight.astype(jnp.float32...  43.8 us
    dot_general x1, matrix products, analyse(): jnp.einsum('svcpl,plk->svcpk', stacked, legendre, precision=HIGHEST)  42.7 us
    mul x1, other arithmetic, inverse_table(): 2.0 * jnp.cos(upper_angle)  29.7 us
    cos x1, other arithmetic, forward_table(): jnp.cos(upper_angle)  28.4 us
    mul x1, other arithmetic, inverse_table(): -lower_scale * jnp.sin(lower_angle)  28.4 us
  transfers between devices with their start and end apart: 6, of which 2 were waited for; matrix products, arithmetic and copies ran while one was open for 26% of the time, Pallas kernels for 0%

profile of v1, /device:TPU:0, one launch (start us, length us, event | category | flops | bytes accessed | tf_op | source)
XLA Modules:
  0.0 634.3 jit_solution(6311171368703555158)
XLA Ops:
  8.7 2.9 collective-permute-start.1
  11.6 28.4 %fusion.32 = (f32[2560,1,640]{2,0,1:T(8,128)}, f32[2560,1,640]{2,0,1:T(8,128)}) fusion(s32[640]{0:T(1024)S(1)} %iota_subtract_fusion), kind=kLoop, calls=%fused_computation.40 | loop fusion | flops 16384000 | bytes 13109760 | tf_op jit(solution)/shard_map/cos | solution.py:33
  40.2 47.9 %copy.114 = bf16[2,160,10,64,32]{3,4,2,1,0:T(8,128)(2,1)} copy(bf16[2,160,10,64,32]{1,4,3,2,0:T(8,128)(2,1)} %param.7) | data formatting | bytes 26214400 | tf_op args[2]
  91.1 3.6 copy.113
  94.7 43.8 %convolution_bitcast_fusion = f32[2,160,2,10,32]{4,2,3,1,0:T(2,128)S(1)} fusion(f32[2,160,2,10,64]{4,2,3,1,0:T(2,128)} %copy.113, bf16[2,160,10,64,32]{3,4,2,1,0:T(8,128)(2,1)} %copy.114), kind=kOutput, calls=%fused_computation.67 | convolution fusion | flops 157286400 | bytes 15564800 | tf_op jit(solution)/shard_map/hlvtj,hltji->hlvti/dot_general | solution.py:100
  138.5 3.4 copy.115
  144.2 3.7 all-to-all-start
  148.0 27.9 %sine_negate_fusion.1 = (f32[2560,1,640]{2,0,1:T(8,128)}, f32[2560,1,640]{2,0,1:T(8,128)}) fusion(), kind=kLoop, calls=%fused_computation.41 | loop fusion | flops 16384000 | bytes 13107200 | tf_op jit(solution)/shard_map/neg | solution.py:33
  176.5 19.3 %fusion.54 = f32[2,2,4,640,20]{3,4,1,0,2:T(8,128)S(1)} fusion(f32[2,20,2,2560,1]{3,1,2,0,4:T(8,128)S(1)} %reshape.511, f32[2560,1,640]{2,0,1:T(8,128)} %get-tuple-element.25, f32[2560,1,640]{2,0,1:T(8,128)} %get-tuple-element.24, f32[2560,1,640]{2,0,1:T(8,128)} %get-tuple-element.30, f32[2560,1,640]{2,0,1:T(8,128)} %get-tuple-element.31), kind=kOutput, calls=%fused_computation.78 | convolution fusion | flops 6317670400 | bytes 27852800 | tf_op jit(solution)/shard_map/hlvn,ncp->hvcpl/dot_general | solution.py:113
  195.8 5.0 copy.120
  200.8 10.6 %reshape.518 = f32[8,1,25600]{2,1,0:T(1,128)} reshape(f32[640,4,2,2,20]{4,3,2,1,0:T(2,128)} %bitcast.91) | data formatting | bytes 1638400
  211.4 4.2 all-to-all-start.1
  216.0 12.5 %all-to-all-done.1 = f32[8,1,25600]{2,1,0:T(1,128)S(1)} async-done(((f32[8,1,25600]{2,1,0:T(1,128)}), f32[8,1,25600]{2,1,0:T(1,128)S(1)}, u32[]{:S(2)}, u32[]{:S(2)}) %all-to-all-start.1) | async-done | bytes 819232 | tf_op jit(solution)/shard_map/all_to_all | solution.py:116
  229.0 2.6 reduce
  231.6 10.9 %reshape.519 = f32[640,4,2,2,20]{4,3,2,1,0:T(2,128)} reshape(f32[8,25600]{1,0:T(8,128)S(1)} %reduce) | data formatting | bytes 1638400
  242.5 6.2 copy.141
  250.4 42.7 %fusion.44 = f32[2,2,4,80,1281]{4,2,1,0,3:T(4,128)} fusion(f32[80,160,1281]{2,1,0:T(8,128)} %param.8, f32[2,2,4,80,160]{4,2,1,0,3:T(4,128)S(1)} %fusion.83), kind=kOutput, calls=%fused_computation.61 | convolution fusion | flops 3148185600 | bytes 72965120 | tf_op jit(solution)/shard_map/svcpl,plk->svcpk/dot_general | solution.py:68
  293.1 4.5 fusion.48
  297.6 2.7 slice_select_fusion
  301.0 28.4 %sine_multiply_fusion.1 = (f32[1,640,2560]{2,1,0:T(8,128)}, f32[1,640,2560]{2,1,0:T(8,128)}) fusion(f32[640]{0:T(1024)S(1)} %fusion.65, f32[640]{0:T(1024)S(1)} %fusion.64), kind=kLoop, calls=%fused_computation.51 | loop fusion | flops 18022400 | bytes 13112320 | tf_op jit(solution)/shard_map/mul | solution.py:48
  329.4 101.4 %all-gather.3.cloned.1.call-done = f32[8,2,80,1281]{3,1,0,2:T(2,128)} async-done(((f32[2,2,80,1281]{3,1,0,2:T(2,128)}), f32[8,2,80,1281]{3,1,0,2:T(2,128)}) %all-gather.3.cloned.1.call-update) | async-done | bytes 6558736 | tf_op jit(solution)/shard_map/all_gather | solution.py:121
  430.8 7.1 %reduce_sum.9 = f32[2,2,80,1281]{3,1,0,2:T(2,128)S(1)} reduce(f32[4,2,2,80,1281]{4,2,1,0,3:T(2,128)} %bitcast.96, f32[]{:T(128)} %constant.78.clone.1), dimensions={0}, to_apply=%region_0.1 | reduce | flops 1229760 | bytes 8198404 | tf_op jit(solution)/shard_map/reduce_sum | solution.py:121
  446.0 73.2 %fusion.49 = f32[2,2,4,80,160]{4,2,1,0,3:T(4,128)S(1)} fusion(f32[80,160,1281]{2,1,0:T(8,128)} %param.8, f32[1,2,4,80,1281]{4,2,1,3,0:T(4,128)S(1)} %negate_select_fusion, f32[1,2,4,80,1281]{4,2,1,3,0:T(4,128)S(1)} %maximum_bitcast_fusion.4), kind=kOutput, calls=%fused_computation.77 | convolution fusion | flops 3149825280 | bytes 72965120 | tf_op jit(solution)/shard_map/hvcpk,plk->hvcpl/dot_general | solution.py:84
  520.8 3.9 all-to-all-start.2
  524.8 29.7 %cosine_multiply_fusion = (f32[1,640,2560]{2,1,0:T(8,128)}, f32[1,640,2560]{2,1,0:T(8,128)}) fusion(s32[640]{0:T(1024)S(1)} %iota_subtract_fusion), kind=kLoop, calls=%fused_computation.47 | loop fusion | flops 18022400 | bytes 13109760 | tf_op jit(solution)/shard_map/mul | solution.py:49
  555.7 19.2 %fusion.47 = f32[2,20,2,2560]{3,1,2,0:T(8,128)S(1)} fusion(f32[2,2,4,640,20]{3,4,2,1,0:T(8,128)S(1)} %reshape.517, f32[1,640,2560]{2,1,0:T(8,128)} %get-tuple-element.23, f32[1,640,2560]{2,1,0:T(8,128)} %get-tuple-element.22, f32[1,640,2560]{2,1,0:T(8,128)} %get-tuple-element.32, f32[1,640,2560]{2,1,0:T(8,128)} %get-tuple-element.33), kind=kOutput, calls=%fused_computation.62 | convolution fusion | flops 6311116800 | bytes 27852800 | tf_op jit(solution)/shard_map/hvcpl,cpn->hlvn/dot_general | solution.py:125
  574.9 4.9 copy.132
  579.9 9.9 %reshape.520 = f32[8,1,25600]{2,1,0:T(1,128)S(1)} reshape(f32[2560,2,2,20]{3,2,1,0:T(2,128)} %bitcast.93) | data formatting | bytes 1638400
  589.8 17.2 %all_to_all.69 = f32[8,1,25600]{2,1,0:T(1,128)S(1)} all-to-all(f32[8,1,25600]{2,1,0:T(1,128)S(1)} %reshape.520), channel_id=1, replica_groups=mesh['band'=4,'sector'=8] {'sector'}, dimensions={0} | all-to-all | bytes 1638400 | tf_op jit(solution)/shard_map/all_to_all | solution.py:131
  607.0 2.6 reduce.1
  609.5 10.9 %reshape.521 = f32[2560,2,2,20]{3,2,1,0:T(2,128)} reshape(f32[8,25600]{1,0:T(8,128)S(1)} %reduce.1) | data formatting | bytes 1638400
  620.4 5.0 copy.144
  (49 shorter events, 23.9 us)
Async XLA Ops:
  8.2 80.0 %collective-permute-start = (f32[2,160,2,96]{1,3,2,0:T(8,128)S(1)}, f32[2,160,2,96]{1,3,2,0:T(8,128)S(1)}, u32[]{:S(2)}, u32[]{:S(2)}) collective-permute-start(f32[2,160,2,96]{1,3,2,0:T(8,128)S(1)} %get-tuple-element.15), channel_id=1, source_target_pairs={{0,1},{1,2},{2,3},{3,4},{4,5},{5,6},{6,7},{7,0},{8,9},{9,10},{10,1... | collective-permute-start | bytes 737288 | tf_op jit(solution)/shard_map/ppermute | solution.py:17
  8.7 79.4 %collective-permute-start.1 = (f32[2,160,2,96]{1,3,2,0:T(8,128)S(1)}, f32[2,160,2,96]{1,3,2,0:T(8,128)S(1)}, u32[]{:S(2)}, u32[]{:S(2)}) collective-permute-start(f32[2,160,2,96]{1,3,2,0:T(8,128)S(1)} %get-tuple-element.16), channel_id=1, source_target_pairs={{1,0},{2,1},{3,2},{4,3},{5,4},{6,5},{7,6},{0,7},{9,8},{10,9},{11,1... | collective-permute-start | bytes 737288 | tf_op jit(solution)/shard_map/ppermute | solution.py:18
  11.6 28.4 %copy-start = (s32[2,160,10]{1,0,2:T(2,128)S(1)}, s32[2,160,10]{1,0,2:T(2,128)}, u32[]{:S(2)}) copy-start(s32[2,160,10]{1,0,2:T(2,128)} %param.6) | copy-start | bytes 38404
  144.2 31.6 %all-to-all-start = ((f32[2,160,2,320]{3,2,0,1:T(2,128)}), f32[2,160,2,320]{3,2,0,1:T(2,128)S(1)}, u32[]{:S(2)}, u32[]{:S(2)}) async-start(f32[2,160,2,320]{3,2,0,1:T(2,128)} %copy.116), calls=%async_computation | async-start | bytes 1966080 | tf_op jit(solution)/shard_map/all_to_all | solution.py:108
  211.4 17.1 %all-to-all-start.1 = ((f32[8,1,25600]{2,1,0:T(1,128)}), f32[8,1,25600]{2,1,0:T(1,128)S(1)}, u32[]{:S(2)}, u32[]{:S(2)}) async-start(f32[8,1,25600]{2,1,0:T(1,128)} %reshape.518), calls=%async_computation.1 | async-start | bytes 1638400 | tf_op jit(solution)/shard_map/all_to_all | solution.py:116
  215.6 215.2 %all-gather.3.cloned.1.call-start = ((), (), s32[]{:S(2)}) async-start(), calls=%async_computation.4 | async-start | bytes 9011200 | tf_op jit(solution)/shard_map/all_gather | solution.py:121
  297.5 3.0 copy-start.1
  520.8 33.6 %all-to-all-start.2 = ((f32[2,2,4,80,160]{3,2,1,0,4:T(4,128)}), f32[2,2,4,80,160]{3,2,1,0,4:T(4,128)S(1)}, u32[]{:S(2)}, u32[]{:S(2)}) async-start(f32[2,2,4,80,160]{3,2,1,0,4:T(4,128)} %copy.128), calls=%async_computation.2 | async-start | bytes 2621440 | tf_op jit(solution)/shard_map/all_to_all | solution.py:124
Sparse Core Ops, SparseCore 0:
  300.4 130.3 all-gather.2
